TPU v7x, 32 devices: a 4x4x1 block of a 4x4x8 slice. The times are simulated.
32 devices in a mesh: dp: 2 (over z, core), ep: 16 (over x, y).
Axes of the slice: x: 4, y: 4, z: 1, core: 2. Of those that a mesh axis runs over, the one named last changes fastest.
The devices are a block of a 4x4x8 slice.
Arguments:
- x: bfloat16 [2, 16, 512, 1280], P('dp', 'ep'), parts along dimension 0
- expert: int32 [2, 16, 512, 1], P('dp', 'ep'), parts along dimension 0
- slot: int32 [2, 16, 512, 1], P('dp', 'ep'), parts along dimension 0
- gate: float32 [2, 16, 512, 1], P('dp', 'ep'), parts along dimension 0
- w_gate: bfloat16 [32, 1280, 8192], P('ep')
- w_up: bfloat16 [32, 1280, 8192], P('ep')
- w_down: bfloat16 [32, 8192, 1280], P('ep')
- s_gate: bfloat16 [1280, 8192], replicated
- s_up: bfloat16 [1280, 8192], replicated
- s_down: bfloat16 [8192, 1280], replicated
Outputs:
- y: bfloat16 [2, 16, 512, 1280], P('dp', 'ep'), parts along dimension 0
There are 2 independent parts. A program takes and returns all parts, laid end to end along the dimension named above; an argument that names none is the same for every part.
All inputs are finite; a program needn't handle non-finite values.
Results may differ from a plain program's by a relative error of at most 0.009.
Values are sent between devices in bfloat16 or wider.
A program may use at most 768 MiB of HBM per device.

v0:
```python
import jax
import jax.numpy as jnp
from jax import lax
from jax.sharding import NamedSharding, PartitionSpec as P


def einsum(form, a, b):
    return jnp.einsum(form, a.astype(jnp.float32), b.astype(jnp.float32))


def for_all(x, s_gate, s_up, s_down):
    h = jax.nn.silu(einsum("...d,df->...f", x, s_gate)) * einsum("...d,df->...f", x, s_up)
    return einsum("...f,fd->...d", h.astype(jnp.bfloat16), s_down)


def solution(mesh):
    def placed(v, *spec):
        return lax.with_sharding_constraint(v, NamedSharding(mesh, P(*spec)))

    def step(x, expert, slot, gate, w_gate, w_up, w_down, s_gate, s_up, s_down):
        experts, (tokens, top) = w_gate.shape[0], expert.shape[2:]
        slots = 5 * tokens * top // (4 * experts)
        to_expert = jax.nn.one_hot(expert, experts, dtype=jnp.bfloat16)
        to_slot = jax.nn.one_hot(slot, slots, dtype=jnp.bfloat16)
        weighted = to_expert * gate[..., None].astype(jnp.bfloat16)
        dispatch = einsum("abtke,abtkc->abtec", to_expert, to_slot).astype(jnp.bfloat16)
        combine = einsum("abtke,abtkc->abtec", weighted, to_slot).astype(jnp.bfloat16)
        z = einsum("abtec,abtd->aebcd", dispatch, x).astype(jnp.bfloat16)
        z = placed(z, "dp", None, "ep", None, None)
        z = placed(z, "dp", "ep", None, None, None)
        h = jax.nn.silu(einsum("aebcd,edf->aebcf", z, w_gate))
        h = (h * einsum("aebcd,edf->aebcf", z, w_up)).astype(jnp.bfloat16)
        out = einsum("aebcf,efd->aebcd", h, w_down).astype(jnp.bfloat16)
        out = placed(out, "dp", "ep", None, None, None)
        out = placed(out, "dp", None, "ep", None, None)
        y = einsum("abtec,aebcd->abtd", combine, out)
        return (y + for_all(x, s_gate, s_up, s_down)).astype(jnp.bfloat16)

    return step
```

profile of v0, /device:TPU:97, one launch (start us, length us, event | category | flops | bytes accessed | tf_op | source)
XLA Modules:
  0.0 196.4 jit_solution(14364507077942131732)
XLA Ops:
  0.0 0.0 copy-start
  0.0 0.0 copy-start.4
  0.0 0.0 copy-start.5
  0.0 0.8 convert_bitcast_fusion
  0.8 0.7 convert_bitcast_fusion.1
  1.5 0.0 copy-start.2
  1.5 0.6 copy-done.2
  2.1 0.0 copy-done
  2.1 2.2 %convolution_convert_fusion = bf16[32,20,1280]{2,0,1:T(8,128)(2,1)} fusion(bf16[1,1,512,1280]{3,2,1,0:T(8,128)(2,1)S(1)} %copy-done, f32[512,32]{0,1:T(8,128)S(1)} %convert_bitcast_fusion, f32[512,20]{0,1:T(8,128)S(1)} %convert_bitcast_fusion.1), kind=kOutput, calls=%fused_computation.26 | convolution fusion | flops 840335360 | bytes 3055616 | tf_op jit(solution)/abtec,abtd->aebcd/dot_general | solution.py:8
  4.3 3.6 %reshape.27 = bf16[1,16,2,1,20,1280]{5,2,1,4,3,0:T(2,128)(2,1)S(1)} reshape(bf16[32,20,1280]{2,0,1:T(8,128)(2,1)} %convolution_convert_fusion) | data formatting | bytes 3276800 | tf_op jit(solution)/sharding_constraint;jit(solution)/sharding_constraint | solution.py:18
  8.0 2.3 %copy.3 = bf16[1,16,2,1,20,1280]{5,2,4,3,0,1:T(2,128)(2,1)} copy(bf16[1,16,2,1,20,1280]{5,2,1,4,3,0:T(2,128)(2,1)S(1)} %reshape.27) | data formatting | bytes 3276800 | tf_op jit(solution)/sharding_constraint;jit(solution)/sharding_constraint | solution.py:18
  10.3 9.5 %all-to-all-start = ((bf16[1,16,2,1,20,1280]{5,2,4,3,0,1:T(2,128)(2,1)}), bf16[1,16,2,1,20,1280]{5,2,4,3,0,1:T(2,128)(2,1)S(1)}, u32[]{:S(2)}, u32[]{:S(2)}) async-start(bf16[1,16,2,1,20,1280]{5,2,4,3,0,1:T(2,128)(2,1)} %copy.3), calls=%async_computation | async-start | bytes 3276800 | tf_op jit(solution)/sharding_constraint;jit(solution)/sharding_constraint | solution.py:18
  19.8 0.0 copy-done.5
  19.9 0.0 copy-done.4
  19.9 0.6 fusion.59
  20.5 20.0 %all-to-all-done = bf16[1,16,2,1,20,1280]{5,2,4,3,0,1:T(2,128)(2,1)S(1)} async-done(((bf16[1,16,2,1,20,1280]{5,2,4,3,0,1:T(2,128)(2,1)}), bf16[1,16,2,1,20,1280]{5,2,4,3,0,1:T(2,128)(2,1)S(1)}, u32[]{:S(2)}, u32[]{:S(2)}) %all-to-all-start) | async-done | bytes 1638432 | tf_op jit(solution)/sharding_constraint;jit(solution)/sharding_constraint | solution.py:18
  40.5 30.2 %fusion.2 = f32[2,16,20,8192]{3,2,1,0:T(8,128)} fusion(bf16[2,1280,8192]{2,1,0:T(8,128)(2,1)} %param.5, bf16[1,16,2,1,20,1280]{5,2,4,3,0,1:T(2,128)(2,1)S(1)} %all-to-all-done), kind=kOutput, calls=%fused_computation.2 | convolution fusion | flops 13421772800 | bytes 64552960 | tf_op jit(solution)/aebcd,edf->aebcf/dot_general | solution.py:8
  70.7 29.9 %fusion.83 = bf16[2,16,20,8192]{3,2,1,0:T(8,128)(2,1)} fusion(f32[2,16,20,8192]{3,2,1,0:T(8,128)} %fusion.2, bf16[2,1280,8192]{2,1,0:T(8,128)(2,1)} %param.4, bf16[1,16,2,1,20,1280]{5,2,4,3,0,1:T(2,128)(2,1)S(1)} %all-to-all-done), kind=kOutput, calls=%fused_computation.20.clone.clone.clone.clone.clone.1 | convolution fusion | flops 13453230080 | bytes 75038720 | tf_op jit(solution)/aebcd,edf->aebcf/dot_general | solution.py:8
  100.6 24.0 %fusion.31 = bf16[1,2,16,1,20,1280]{5,4,2,1,3,0:T(8,128)(2,1)S(1)} fusion(bf16[2,8192,1280]{2,1,0:T(8,128)(2,1)} %param.6, bf16[2,16,20,8192]{3,2,1,0:T(8,128)(2,1)} %fusion.83), kind=kOutput, calls=%fused_computation.28 | convolution fusion | flops 13422592000 | bytes 54067200 | tf_op jit(solution)/aebcf,efd->aebcd/dot_general | solution.py:8
  124.6 2.9 %copy.5 = bf16[1,2,16,1,20,1280]{5,1,4,3,0,2:T(2,128)(2,1)} copy(bf16[1,2,16,1,20,1280]{5,4,2,1,3,0:T(8,128)(2,1)S(1)} %fusion.31) | data formatting | bytes 3276800 | tf_op jit(solution)/sharding_constraint;jit(solution)/sharding_constraint | solution.py:18
  127.5 6.6 %all-to-all-start.1 = ((bf16[1,2,16,1,20,1280]{5,1,4,3,0,2:T(2,128)(2,1)}), bf16[1,2,16,1,20,1280]{5,1,4,3,0,2:T(2,128)(2,1)S(1)}, u32[]{:S(2)}, u32[]{:S(2)}) async-start(bf16[1,2,16,1,20,1280]{5,1,4,3,0,2:T(2,128)(2,1)} %copy.5), calls=%async_computation.1 | async-start | bytes 3276800 | tf_op jit(solution)/sharding_constraint;jit(solution)/sharding_constraint | solution.py:18
  134.1 0.0 copy-start.1
  134.1 0.0 copy-start.3
  134.1 18.4 %fusion.46 = f32[512,8192]{1,0:T(8,128)} fusion(bf16[1280,8192]{1,0:T(8,128)(2,1)} %param.7, bf16[1,1,512,1280]{3,2,1,0:T(8,128)(2,1)S(1)} %copy-done), kind=kOutput, calls=%fused_computation.35 | convolution fusion | flops 10737418240 | bytes 39059456 | tf_op jit(solution)/...d,df->...f/dot_general | solution.py:8
  152.5 2.9 %all-to-all-done.1 = bf16[1,2,16,1,20,1280]{5,1,4,3,0,2:T(2,128)(2,1)S(1)} async-done(((bf16[1,2,16,1,20,1280]{5,1,4,3,0,2:T(2,128)(2,1)}), bf16[1,2,16,1,20,1280]{5,1,4,3,0,2:T(2,128)(2,1)S(1)}, u32[]{:S(2)}, u32[]{:S(2)}) %all-to-all-start.1) | async-done | bytes 1638432 | tf_op jit(solution)/sharding_constraint;jit(solution)/sharding_constraint | solution.py:18
  155.4 2.8 %copy.6 = bf16[1,16,2,1,20,1280]{5,2,1,4,3,0:T(2,128)(2,1)} copy(bf16[1,16,2,1,20,1280]{5,2,4,3,0,1:T(2,128)(2,1)S(1)} %bitcast.180) | data formatting | bytes 3276800 | tf_op jit(solution)/sharding_constraint;jit(solution)/sharding_constraint | solution.py:18
  158.3 3.8 %reshape.64 = bf16[32,20,1280]{2,0,1:T(8,128)(2,1)S(1)} reshape(bf16[1,16,2,1,20,1280]{5,2,1,4,3,0:T(2,128)(2,1)} %copy.6) | data formatting | bytes 3276800
  162.1 0.0 copy-done.1
  162.1 0.0 copy-done.3
  162.1 2.7 %convolution_bitcast_fusion = f32[512,1280]{1,0:T(8,128)} fusion(bf16[32,20,1280]{2,0,1:T(8,128)(2,1)S(1)} %reshape.64, f32[512,20]{0,1:T(8,128)S(1)} %copy-done.3, f32[512,32]{0,1:T(8,128)S(1)} %copy-done.1), kind=kOutput, calls=%fused_computation.25 | convolution fusion | flops 839516160 | bytes 4366336 | tf_op jit(solution)/abtec,aebcd->abtd/dot_general | solution.py:8
  164.8 31.6 %fusion.38 = bf16[1,1,512,1280]{3,2,1,0:T(8,128)(2,1)} fusion(f32[512,1280]{1,0:T(8,128)} %convolution_bitcast_fusion, bf16[8192,1280]{1,0:T(8,128)(2,1)} %param.9, bf16[1280,8192]{1,0:T(8,128)(2,1)} %param.8, f32[512,8192]{1,0:T(8,128)} %fusion.46, bf16[1,1,512,1280]{3,2,1,0:T(8,128)(2,1)S(1)} %copy-done), kind=kOutput, calls=%fused_computation.29 | convolution fusion | flops 21501313024 | bytes 63963136 | tf_op jit(solution)/...f,fd->...d/dot_general | solution.py:8
  (1 shorter events, 0.0 us)
Async XLA Ops:
  0.0 2.1 %copy-start = (bf16[1,1,512,1280]{3,2,1,0:T(8,128)(2,1)S(1)}, bf16[1,1,512,1280]{3,2,1,0:T(8,128)(2,1)}, u32[]{:S(2)}) copy-start(bf16[1,1,512,1280]{3,2,1,0:T(8,128)(2,1)} %param.3) | copy-start | bytes 3932164
  0.0 19.9 %copy-start.4 = (s32[1,1,512,1]{2,3,1,0:T(1,128)S(1)}, s32[1,1,512,1]{2,3,1,0:T(1,128)}, u32[]{:S(2)}) copy-start(s32[1,1,512,1]{2,3,1,0:T(1,128)} %param) | copy-start | bytes 6148
  0.0 19.8 %copy-start.5 = (f32[1,1,512,1]{2,3,1,0:T(1,128)S(1)}, f32[1,1,512,1]{2,3,1,0:T(1,128)}, u32[]{:S(2)}) copy-start(f32[1,1,512,1]{2,3,1,0:T(1,128)} %param.1) | copy-start | bytes 6148
  1.5 0.6 copy-start.2
  10.3 30.2 %all-to-all-start = ((bf16[1,16,2,1,20,1280]{5,2,4,3,0,1:T(2,128)(2,1)}), bf16[1,16,2,1,20,1280]{5,2,4,3,0,1:T(2,128)(2,1)S(1)}, u32[]{:S(2)}, u32[]{:S(2)}) async-start(bf16[1,16,2,1,20,1280]{5,2,4,3,0,1:T(2,128)(2,1)} %copy.3), calls=%async_computation | async-start | bytes 3276800 | tf_op jit(solution)/sharding_constraint;jit(solution)/sharding_constraint | solution.py:18
  127.5 27.9 %all-to-all-start.1 = ((bf16[1,2,16,1,20,1280]{5,1,4,3,0,2:T(2,128)(2,1)}), bf16[1,2,16,1,20,1280]{5,1,4,3,0,2:T(2,128)(2,1)S(1)}, u32[]{:S(2)}, u32[]{:S(2)}) async-start(bf16[1,2,16,1,20,1280]{5,1,4,3,0,2:T(2,128)(2,1)} %copy.5), calls=%async_computation.1 | async-start | bytes 3276800 | tf_op jit(solution)/sharding_constraint;jit(solution)/sharding_constraint | solution.py:18
  134.1 27.9 %copy-start.1 = (f32[512,32]{0,1:T(8,128)S(1)}, f32[512,32]{0,1:T(8,128)}, u32[]{:S(2)}) copy-start(f32[512,32]{0,1:T(8,128)} %fusion.59) | copy-start | bytes 196612
  134.1 27.9 %copy-start.3 = (f32[512,20]{0,1:T(8,128)S(1)}, f32[512,20]{0,1:T(8,128)}, u32[]{:S(2)}) copy-start(f32[512,20]{0,1:T(8,128)} %copy-done.2) | copy-start | bytes 122884
where the time goes:
time: 198 us; the launch traced here: 196 us
  matrix products  139 us (70%)
  waiting for transfers between devices  22.9 us (12%)
  starting transfers between devices  16.2 us (8%)
  local copies, waits for them, and re-layouts  16.1 us (8%)
  other arithmetic  2.15 us (1%)
    dot_general x7, matrix products, einsum(): return jnp.einsum(form, a.astype(jnp.float32), b.astype(jnp.float32))  139 us
    another operation x2, waiting for transfers between devices, placed(): return lax.with_sharding_constraint(v, NamedSharding(mesh, P(*spec)))  22.9 us
    another operation x2, starting transfers between devices, placed(): return lax.with_sharding_constraint(v, NamedSharding(mesh, P(*spec)))  16.2 us
    another operation x4, local copies, waits for them, and re-layouts, placed(): return lax.with_sharding_constraint(v, NamedSharding(mesh, P(*spec)))  11.6 us
    unnamed x13, local copies, waits for them, and re-layouts  4.44 us
  transfers between devices with their start and end apart: 2, of which 2 were waited for; matrix products, arithmetic and copies ran while one was open for 10% of the time, Pallas kernels for 0%

commit v1 on v0

v1 whole, which is shorter than its diff:
```python
import functools

import jax
import jax.numpy as jnp
from jax import lax
from jax.experimental import pallas as pl
from jax.experimental.pallas import tpu as pltpu
from jax.sharding import PartitionSpec as P

F32, BF16 = jnp.float32, jnp.bfloat16
TILE = 512
UNROLL = 4
RING = 10
LEAD = 8
COL = 256


def kernel(
    n, slots, steps,
    x_hbm, expert, slot, gate, wg, wu, wd, sg, su, sd, y_hbm,
    x_v, zsend, zrecv, z_v, osend, orecv, acc_s, acc_r, h0, h1, bg, bu, bd,
    x_sem, w_sem, zs_sem, zr_sem, os_sem, or_sem, y_sem,
):
    me = lax.axis_index("ep")
    tokens, width = x_v.shape
    local = wg.shape[0]
    block = zsend.shape[2]
    routed = local * steps
    total = routed + steps
    parity = lax.rem(me, 2)

    barrier = pltpu.get_barrier_semaphore()

    def greet(o, c):
        pl.semaphore_signal(barrier, inc=1, device_id={"ep": lax.rem(me + o, n)})
        return c

    lax.fori_loop(1, n, greet, 0)
    x_copy = pltpu.make_async_copy(x_hbm, x_v, x_sem)
    x_copy.start()

    def copies(at, gate_w, up_w, down_w, column):
        cols = pl.ds(pl.multiple_of(column * TILE, TILE), TILE)
        return (
            pltpu.make_async_copy(gate_w.at[:, cols], bg.at[at], w_sem.at[at, 0]),
            pltpu.make_async_copy(up_w.at[:, cols], bu.at[at], w_sem.at[at, 1]),
            pltpu.make_async_copy(down_w.at[cols, :], bd.at[at], w_sem.at[at, 2]),
        )

    def fetch(s):
        at = lax.rem(s, RING)
        before, after = s < LEAD, s >= LEAD + routed

        @pl.when(jnp.logical_and(jnp.logical_or(before, after), s < total))
        def _():
            column = jnp.where(before, s, s - routed)
            for c in copies(at, sg, su, sd, column):
                c.start()

        @pl.when(jnp.logical_not(jnp.logical_or(before, after)))
        def _():
            r = s - LEAD
            e = r // steps
            for c in copies(at, wg.at[e], wu.at[e], wd.at[e], lax.rem(r, steps)):
                c.start()

    def prefill(s, c):
        fetch(s)
        return c

    lax.fori_loop(0, RING - UNROLL, prefill, 0)

    def target():
        e, s = expert[...], slot[...]
        row = lax.rem(e, local) * (n * block) + (e // local) * block + s + 4 * parity
        return jnp.where(s < slots, row, -1)

    def dispatch(j):
        rows = lax.broadcasted_iota(jnp.int32, (n * block, tokens), 0) + j * (n * block)
        pick = jnp.where(rows == target(), 1.0, 0.0).astype(BF16)
        z = jnp.dot(pick, x_v[...], preferred_element_type=F32)
        for d in range(n):
            zsend[j, d] = z[d * block : (d + 1) * block].astype(BF16)

    def exchange(j, o, src, dst, s_sem, r_sem):
        to = lax.rem(me + o, n)
        return pltpu.make_async_remote_copy(
            src_ref=src.at[j, to],
            dst_ref=dst.at[j, me],
            send_sem=s_sem.at[j, o],
            recv_sem=r_sem.at[j, o],
            device_id={"ep": to},
        )

    def arrive(j, o, src, dst, s_sem, r_sem):
        frm = lax.rem(me + n - o, n)
        return pltpu.make_async_remote_copy(
            src_ref=src.at[j, frm],
            dst_ref=dst.at[j, frm],
            send_sem=s_sem.at[j, o],
            recv_sem=r_sem.at[j, o],
            device_id={"ep": frm},
        )

    def send_all(j, *refs):
        def one(o, c):
            exchange(j, o, *refs).start()
            return c

        lax.fori_loop(1, n, one, 0)
        src, dst = refs[:2]
        dst[j, me] = src[j, me]

    def wait_all(j, *refs):
        def one(o, c):
            arrive(j, o, *refs).wait_recv()
            return c

        lax.fori_loop(1, n, one, 0)

    def sent_all(j, *refs):
        def one(o, c):
            exchange(j, o, *refs).wait_send()
            return c

        lax.fori_loop(1, n, one, 0)

    z_refs = (zsend, zrecv, zs_sem, zr_sem)
    o_refs = (osend, orecv, os_sem, or_sem)

    x_copy.wait()
    for j in range(local):
        dispatch(j)
    pl.semaphore_wait(barrier, n - 1)
    for j in range(local):
        send_all(j, *z_refs)

    hs = (h0, h1)

    def run(base, rows, lhs, acc):
        ats = [lax.rem(base + k, RING) for k in range(UNROLL)]
        for k in range(UNROLL):
            for c in copies(ats[k], sg, su, sd, 0):
                c.wait()
        for k in range(UNROLL):
            fetch(base + (RING - UNROLL) + k)
        for k in range(UNROLL + 1):
            if k < UNROLL:
                h = hs[k % 2]
                for a in range(0, TILE, COL):
                    g = jnp.dot(lhs[...], bg[ats[k], :, a : a + COL], preferred_element_type=F32)
                    u = jnp.dot(lhs[...], bu[ats[k], :, a : a + COL], preferred_element_type=F32)
                    h[:rows, a : a + COL] = (jax.nn.silu(g) * u).astype(BF16)
            if k > 0:
                h = hs[(k - 1) % 2]
                for a in range(0, width, COL):
                    acc[:, a : a + COL] += jnp.dot(
                        h[:rows, :], bd[ats[k - 1], :, a : a + COL], preferred_element_type=F32
                    )

    def shared(i, c):
        run(i * UNROLL, tokens, x_v, acc_s)
        return c

    acc_s[...] = jnp.zeros_like(acc_s)
    lax.fori_loop(0, LEAD // UNROLL, shared, 0)

    rows = n * slots

    def one_expert(j, c):
        wait_all(j, *z_refs)
        for q in range(0, n, 4):
            parts = []
            for p in (q, q + 2):
                even, odd = zrecv[j, p].astype(F32), zrecv[j, p + 1].astype(F32)
                parts += [even[:16], even[16:] + odd[:8], odd[8:]]
            z_v[q * slots : (q + 4) * slots, :] = jnp.concatenate(parts, axis=0).astype(BF16)
        acc_r[...] = jnp.zeros_like(acc_r)

        def part(i, c):
            run(LEAD + j * steps + i * UNROLL, rows, z_v, acc_r)
            return c

        lax.fori_loop(0, steps // UNROLL, part, 0)
        for d in range(n):
            first = d * slots // 8 * 8
            osend[j, d] = acc_r[first : first + block, :].astype(BF16)
        send_all(j, *o_refs)
        return c

    lax.fori_loop(0, local, one_expert, 0)

    def combine(j):
        wait_all(j, *o_refs)
        at = lax.broadcasted_iota(jnp.int32, (n * block, tokens), 0) + j * (n * block)
        weight = gate[...].astype(BF16).astype(F32)
        pick = jnp.where(at == target(), weight, 0.0).astype(BF16)
        out = jnp.concatenate([orecv[j, d].astype(F32) for d in range(n)], axis=0).astype(BF16)
        return lax.dot_general(pick, out, (((0,), (0,)), ((), ())), preferred_element_type=F32)

    for j in range(local - 1):
        acc_s[...] += combine(j)

    def tail(i, c):
        run(LEAD + routed + i * UNROLL, tokens, x_v, acc_s)
        return c

    lax.fori_loop(0, (steps - LEAD) // UNROLL, tail, 0)

    x_v[...] = (acc_s[...] + combine(local - 1)).astype(BF16)
    y_copy = pltpu.make_async_copy(x_v, y_hbm, y_sem)
    y_copy.start()
    for j in range(local):
        sent_all(j, *z_refs)
        sent_all(j, *o_refs)
    y_copy.wait()


def solution(mesh):
    n = mesh.shape["ep"]

    def part(x, expert, slot, gate, wg, wu, wd, sg, su, sd):
        tokens, width = x.shape[2:]
        local, _, hidden = wg.shape
        slots = 5 * tokens * expert.shape[-1] // (4 * local * n)
        block = slots + 4
        assert slots % 8 == 4 and hidden == sg.shape[1]
        steps = hidden // TILE
        hbm = pl.BlockSpec(memory_space=pl.ANY)
        vmem = pl.BlockSpec(memory_space=pltpu.VMEM)
        flops = 6 * width * hidden * (tokens + local * n * slots)
        y = pl.pallas_call(
            functools.partial(kernel, n, slots, steps),
            out_shape=jax.ShapeDtypeStruct((tokens, width), BF16),
            in_specs=[hbm, vmem, vmem, vmem] + [hbm] * 6,
            out_specs=hbm,
            scratch_shapes=[
                pltpu.VMEM((tokens, width), BF16),
                pltpu.VMEM((local, n, block, width), BF16),
                pltpu.VMEM((local, n, block, width), BF16),
                pltpu.VMEM((n * slots, width), BF16),
                pltpu.VMEM((local, n, block, width), BF16),
                pltpu.VMEM((local, n, block, width), BF16),
                pltpu.VMEM((tokens, width), F32),
                pltpu.VMEM((n * slots, width), F32),
                pltpu.VMEM((tokens, TILE), BF16),
                pltpu.VMEM((tokens, TILE), BF16),
                pltpu.VMEM((RING, width, TILE), BF16),
                pltpu.VMEM((RING, width, TILE), BF16),
                pltpu.VMEM((RING, TILE, width), BF16),
                pltpu.SemaphoreType.DMA,
                pltpu.SemaphoreType.DMA((RING, 3)),
                pltpu.SemaphoreType.DMA((local, n)),
                pltpu.SemaphoreType.DMA((local, n)),
                pltpu.SemaphoreType.DMA((local, n)),
                pltpu.SemaphoreType.DMA((local, n)),
                pltpu.SemaphoreType.DMA,
            ],
            compiler_params=pltpu.CompilerParams(
                collective_id=0, has_side_effects=True, vmem_limit_bytes=67043328
            ),
            cost_estimate=pl.CostEstimate(flops=flops, bytes_accessed=6 * width * hidden * (1 + local), transcendentals=0),
            name="moe",
        )(
            x.reshape(tokens, width),
            expert.reshape(1, tokens),
            slot.reshape(1, tokens),
            gate.reshape(1, tokens),
            wg, wu, wd, sg, su, sd,
        )
        return y.reshape(x.shape)

    a, e, s = P("dp", "ep"), P("ep"), P()
    return jax.shard_map(
        part,
        mesh=mesh,
        in_specs=(a, a, a, a, e, e, e, s, s, s),
        out_specs=a,
        check_vma=False,
    )
```

time: 198 us -> 95.3 us (0.48)
  matrix products: 139 us -> 0 us
  Pallas kernels: 0 us -> 92.7 us
  waiting for transfers between devices: 22.9 us -> 0 us
  starting transfers between devices: 16.2 us -> 0 us
  local copies, waits for them, and re-layouts: 16.1 us -> 2.46 us
  other arithmetic: 2.15 us -> 0 us
    dot_general x7 -> x0, matrix products: 139 us -> none  [einsum(): return jnp.einsum(form, a.astype(jnp.float32), b.astype(jnp.float32))]
    pallas_call x0 -> x1, Pallas kernels: none -> 92.7 us  [part(): pl.pallas_call(functools.partial(kernel, n, slots, steps), out_shape=jax....]
    another operation x2 -> x0, waiting for transfers between devices: 22.9 us -> none  [placed(): return lax.with_sharding_constraint(v, NamedSharding(mesh, P(*spec)))]
    another operation x2 -> x0, starting transfers between devices: 16.2 us -> none  [placed(): return lax.with_sharding_constraint(v, NamedSharding(mesh, P(*spec)))]
    another operation x4 -> x0, local copies, waits for them, and re-layouts: 11.6 us -> none  [placed(): return lax.with_sharding_constraint(v, NamedSharding(mesh, P(*spec)))]
    unnamed x3 -> x0, other arithmetic: 2.13 us -> none
    unnamed x13 -> x1, local copies, waits for them, and re-layouts: 4.44 us -> 2.46 us
  transfers between devices with their start and end apart: 2 -> 0, of which waited for: 2 -> 0; matrix products, arithmetic and copies ran while one was open for 10% -> 0% of each run, Pallas kernels for 0% -> 0%
where the time goes in v1:
time: 95.3 us; the launch traced here: 95.2 us
  Pallas kernels  92.7 us (97%)
  local copies, waits for them, and re-layouts  2.46 us (3%)
    pallas_call x1, Pallas kernels, part(): pl.pallas_call(functools.partial(kernel, n, slots, steps), out_shape=jax....  92.7 us
    unnamed x1, local copies, waits for them, and re-layouts  2.46 us

profile of v1, /device:TPU:97, one launch (start us, length us, event | category | flops | bytes accessed | tf_op | source)
XLA Modules:
  0.0 95.2 jit_solution(4892450975525644897)
XLA Ops:
  0.0 92.7 %moe.1 = bf16[512,1280]{1,0:T(8,128)(2,1)} custom-call(bf16[512,1280]{1,0:T(8,128)(2,1)} %bitcast.6, s32[1,512]{1,0:T(1,128)} %bitcast.7, s32[1,512]{1,0:T(1,128)} %bitcast.8, f32[1,512]{1,0:T(1,128)} %bitcast.9, bf16[2,1280,8192]{2,1,0:T(8,128)(2,1)} %wg.1, bf16[2,1280,8192]{2,1,0:T(8,128)(2,1)} %wu.1, bf16[2,8192,1280]{2,1,0:T(8,128)(2,1)} %wd.1, ...), custom_call_target="tpu_custom_call" | custom-call | flops 72477573120 | bytes 188743680 | tf_op jit(solution)/shard_map/moe/pallas_call | solution.py:232
  92.7 2.5 %copy.12 = bf16[1,1,512,1280]{3,2,1,0:T(8,128)(2,1)} copy(bf16[1,1,512,1280]{3,2,1,0:T(8,128)(2,1)} %bitcast.5) | data formatting | bytes 2621440

commit v2 on v1

--- a/solution.py
+++ b/solution.py
@@ -1,4 +1,5 @@
 import functools
+import math
 
 import jax
 import jax.numpy as jnp
@@ -9,10 +10,15 @@
 
 F32, BF16 = jnp.float32, jnp.bfloat16
 TILE = 512
-UNROLL = 4
+SHORT, LONG = 2, 4
 RING = 10
 LEAD = 8
 COL = 256
+VMEM = 62 << 20
+
+
+def ahead(step, ring):
+    return step if 2 * step <= ring else 0
 
 
 def kernel(
@@ -68,7 +74,7 @@
         fetch(s)
         return c
 
-    lax.fori_loop(0, RING - UNROLL, prefill, 0)
+    lax.fori_loop(0, RING, prefill, 0)
 
     def target():
         e, s = expert[...], slot[...]
@@ -82,8 +88,16 @@
         for d in range(n):
             zsend[j, d] = z[d * block : (d + 1) * block].astype(BF16)
 
+    side = math.isqrt(n)
+    side = side if side * side == n else 1
+    far = sorted(range(1, n), key=lambda o: (-ahead(o // side, n // side) - ahead(o % side, side), o))
+
+    def peer(o, sign):
+        i = lax.rem(me // side + n // side + sign * (o // side), n // side)
+        return i * side + lax.rem(lax.rem(me, side) + side + sign * (o % side), side)
+
     def exchange(j, o, src, dst, s_sem, r_sem):
-        to = lax.rem(me + o, n)
+        to = peer(o, 1)
         return pltpu.make_async_remote_copy(
             src_ref=src.at[j, to],
             dst_ref=dst.at[j, me],
@@ -93,7 +107,7 @@
         )
 
     def arrive(j, o, src, dst, s_sem, r_sem):
-        frm = lax.rem(me + n - o, n)
+        frm = peer(o, -1)
         return pltpu.make_async_remote_copy(
             src_ref=src.at[j, frm],
             dst_ref=dst.at[j, frm],
@@ -103,49 +117,35 @@
         )
 
     def send_all(j, *refs):
-        def one(o, c):
+        for o in far:
             exchange(j, o, *refs).start()
-            return c
-
-        lax.fori_loop(1, n, one, 0)
         src, dst = refs[:2]
         dst[j, me] = src[j, me]
 
     def wait_all(j, *refs):
-        def one(o, c):
+        for o in far:
             arrive(j, o, *refs).wait_recv()
-            return c
-
-        lax.fori_loop(1, n, one, 0)
 
     def sent_all(j, *refs):
-        def one(o, c):
+        for o in far:
             exchange(j, o, *refs).wait_send()
-            return c
-
-        lax.fori_loop(1, n, one, 0)
 
     z_refs = (zsend, zrecv, zs_sem, zr_sem)
     o_refs = (osend, orecv, os_sem, or_sem)
 
     x_copy.wait()
-    for j in range(local):
-        dispatch(j)
-    pl.semaphore_wait(barrier, n - 1)
-    for j in range(local):
-        send_all(j, *z_refs)
+    dispatch(0)
 
     hs = (h0, h1)
 
-    def run(base, rows, lhs, acc):
-        ats = [lax.rem(base + k, RING) for k in range(UNROLL)]
-        for k in range(UNROLL):
+    def run(base, count, freed, rows, lhs, acc):
+        ats = [lax.rem(base + k, RING) for k in range(count)]
+        lax.fori_loop(base + RING - freed, base + RING, prefill, 0)
+        for k in range(count):
             for c in copies(ats[k], sg, su, sd, 0):
                 c.wait()
-        for k in range(UNROLL):
-            fetch(base + (RING - UNROLL) + k)
-        for k in range(UNROLL + 1):
-            if k < UNROLL:
+        for k in range(count + 1):
+            if k < count:
                 h = hs[k % 2]
                 for a in range(0, TILE, COL):
                     g = jnp.dot(lhs[...], bg[ats[k], :, a : a + COL], preferred_element_type=F32)
@@ -159,16 +159,27 @@
                     )
 
     def shared(i, c):
-        run(i * UNROLL, tokens, x_v, acc_s)
+        run(2 + i * SHORT, SHORT, jnp.where(i == 0, 1, SHORT), tokens, x_v, acc_s)
         return c
 
     acc_s[...] = jnp.zeros_like(acc_s)
-    lax.fori_loop(0, LEAD // UNROLL, shared, 0)
+    run(0, 1, 0, tokens, x_v, acc_s)
+    pl.semaphore_wait(barrier, n - 1)
+    send_all(0, *z_refs)
+    for j in range(1, local):
+        dispatch(j)
+    run(1, 1, 1, tokens, x_v, acc_s)
+    lax.fori_loop(0, (LEAD - 2) // SHORT, shared, 0)
 
     rows = n * slots
 
     def one_expert(j, c):
         wait_all(j, *z_refs)
+
+        @pl.when(j + 1 < local)
+        def _():
+            send_all(j + 1, *z_refs)
+
         for q in range(0, n, 4):
             parts = []
             for p in (q, q + 2):
@@ -178,10 +189,11 @@
         acc_r[...] = jnp.zeros_like(acc_r)
 
         def part(i, c):
-            run(LEAD + j * steps + i * UNROLL, rows, z_v, acc_r)
+            freed = jnp.where(jnp.logical_and(i == 0, j == 0), SHORT, LONG)
+            run(LEAD + j * steps + i * LONG, LONG, freed, rows, z_v, acc_r)
             return c
 
-        lax.fori_loop(0, steps // UNROLL, part, 0)
+        lax.fori_loop(0, steps // LONG, part, 0)
         for d in range(n):
             first = d * slots // 8 * 8
             osend[j, d] = acc_r[first : first + block, :].astype(BF16)
@@ -190,30 +202,36 @@
 
     lax.fori_loop(0, local, one_expert, 0)
 
-    def combine(j):
+    def returned(j):
         wait_all(j, *o_refs)
+        return jnp.concatenate([orecv[j, d].astype(F32) for d in range(n)], axis=0).astype(BF16)
+
+    def combine(j, out, cols):
         at = lax.broadcasted_iota(jnp.int32, (n * block, tokens), 0) + j * (n * block)
         weight = gate[...].astype(BF16).astype(F32)
-        pick = jnp.where(at == target(), weight, 0.0).astype(BF16)
-        out = jnp.concatenate([orecv[j, d].astype(F32) for d in range(n)], axis=0).astype(BF16)
+        pick = jnp.where(at == target(), weight, 0.0).astype(BF16)[:, cols]
         return lax.dot_general(pick, out, (((0,), (0,)), ((), ())), preferred_element_type=F32)
 
     for j in range(local - 1):
-        acc_s[...] += combine(j)
+        acc_s[...] += combine(j, returned(j), slice(None))
 
     def tail(i, c):
-        run(LEAD + routed + i * UNROLL, tokens, x_v, acc_s)
-        return c
-
-    lax.fori_loop(0, (steps - LEAD) // UNROLL, tail, 0)
-
-    x_v[...] = (acc_s[...] + combine(local - 1)).astype(BF16)
-    y_copy = pltpu.make_async_copy(x_v, y_hbm, y_sem)
-    y_copy.start()
+        run(LEAD + routed + i * LONG, LONG, LONG, tokens, x_v, acc_s)
+        return c
+
+    lax.fori_loop(0, (steps - LEAD) // LONG, tail, 0)
+
+    last, half, y_copies = returned(local - 1), tokens // 2, []
+    for i in range(2):
+        part = slice(i * half, (i + 1) * half)
+        x_v[part, :] = (acc_s[part, :] + combine(local - 1, last, part)).astype(BF16)
+        y_copies.append(pltpu.make_async_copy(x_v.at[part], y_hbm.at[part], y_sem.at[i]))
+        y_copies[i].start()
     for j in range(local):
         sent_all(j, *z_refs)
         sent_all(j, *o_refs)
-    y_copy.wait()
+    for c in y_copies:
+        c.wait()
 
 
 def solution(mesh):
@@ -254,10 +272,10 @@
                 pltpu.SemaphoreType.DMA((local, n)),
                 pltpu.SemaphoreType.DMA((local, n)),
                 pltpu.SemaphoreType.DMA((local, n)),
-                pltpu.SemaphoreType.DMA,
+                pltpu.SemaphoreType.DMA((2,)),
             ],
             compiler_params=pltpu.CompilerParams(
-                collective_id=0, has_side_effects=True, vmem_limit_bytes=67043328
+                collective_id=0, has_side_effects=True, vmem_limit_bytes=VMEM
             ),
             cost_estimate=pl.CostEstimate(flops=flops, bytes_accessed=6 * width * hidden * (1 + local), transcendentals=0),
             name="moe",

time: 95.3 us -> 93.3 us (0.979)
  Pallas kernels: 92.7 us -> 90.7 us
    pallas_call x1, Pallas kernels: 92.7 us -> 90.7 us  [part(): pl.pallas_call(functools.partial(kernel, n, slots, steps), out_shape=jax....]
where the time goes in v2:
time: 93.3 us; the launch traced here: 93.1 us
  Pallas kernels  90.7 us (97%)
  local copies, waits for them, and re-layouts  2.46 us (3%)
    pallas_call x1, Pallas kernels, part(): pl.pallas_call(functools.partial(kernel, n, slots, steps), out_shape=jax....  90.7 us
    unnamed x1, local copies, waits for them, and re-layouts  2.46 us

profile of v2, /device:TPU:97, one launch (start us, length us, event | category | flops | bytes accessed | tf_op | source)
XLA Modules:
  0.0 93.1 jit_solution(312103337698911352)
XLA Ops:
  0.0 90.7 %moe.1 = bf16[512,1280]{1,0:T(8,128)(2,1)} custom-call(bf16[512,1280]{1,0:T(8,128)(2,1)} %bitcast.6, s32[1,512]{1,0:T(1,128)} %bitcast.7, s32[1,512]{1,0:T(1,128)} %bitcast.8, f32[1,512]{1,0:T(1,128)} %bitcast.9, bf16[2,1280,8192]{2,1,0:T(8,128)(2,1)} %wg.1, bf16[2,1280,8192]{2,1,0:T(8,128)(2,1)} %wu.1, bf16[2,8192,1280]{2,1,0:T(8,128)(2,1)} %wd.1, ...), custom_call_target="tpu_custom_call" | custom-call | flops 72477573120 | bytes 188743680 | tf_op jit(solution)/shard_map/moe/pallas_call | solution.py:250
  90.7 2.5 %copy.12 = bf16[1,1,512,1280]{3,2,1,0:T(8,128)(2,1)} copy(bf16[1,1,512,1280]{3,2,1,0:T(8,128)(2,1)} %bitcast.5) | data formatting | bytes 2621440
